TPU v7x, 32 devices: a whole 2x2x4 slice. The times are simulated.
32 devices in a mesh: dp: 4 (over x, core), ctx: 8 (over z, y).
Axes of the slice: x: 2, y: 2, z: 4, core: 2. Of those that a mesh axis runs over, the one named last changes fastest.
Arguments:
- tokens: bfloat16 [4096, 1792], P(('dp', 'ctx')), may hold values from -6 to 6
- cotangent: bfloat16 [4096, 1792], P(('dp', 'ctx')), may hold values from -6 to 6
- expert_ids: int32 [4096, 4], P(('dp', 'ctx')), may hold values from 0 to 15, all different within a row; in each aligned block of 128 rows (0 to 127, 128 to 255, ...) at most 40 rows name the same one
- norm_gain: float32 [1792], replicated, may hold values from 0.5 to 1.5
- router_weight: bfloat16 [1792, 16], replicated, may hold values from -0.125 to 0.125
- gate_weight: bfloat16 [16, 1792, 1536], P('ctx', None, 'dp'), may hold values from -0.125 to 0.125
- up_weight: bfloat16 [16, 1792, 1536], P('ctx', None, 'dp'), may hold values from -0.125 to 0.125
- down_weight: bfloat16 [16, 1536, 1792], P('ctx', 'dp'), may hold values from -0.15625 to 0.15625
Outputs:
- grad_tokens: bfloat16 [4096, 1792], P(('dp', 'ctx'))
- grad_gate: bfloat16 [16, 1792, 1536], P('ctx', None, 'dp')
- grad_up: bfloat16 [16, 1792, 1536], P('ctx', None, 'dp')
- grad_down: bfloat16 [16, 1536, 1792], P('ctx', 'dp')
- grad_router: float32 [1792, 16], P(('dp', 'ctx'))
- grad_gain: float32 [1792], P(('dp', 'ctx'))
Inputs may be any that keep to these rules, and one draw needn't show every extreme that they name: `expert_ids`: each row names 4 different experts; among the rows of one device no expert is named more than 40 times.
All inputs are finite; a program needn't handle non-finite values.
Results may differ from a plain program's by a relative error of at most 0.02.
Values may be sent and summed in bfloat16 or wider, within the bound.
A program may use at most 192 MiB of HBM per device.

v0:
```python
import jax
import jax.numpy as jnp
from jax import lax
from jax.sharding import PartitionSpec as P

EPSILON = 1e-05
SWISH_SCALE = 1.702


def expert_pass(rows, upstream, weight, gate_weight, up_weight, down_weight):
    gate_pre = jnp.einsum("prd,pdf->prf", rows, gate_weight, preferred_element_type=jnp.float32)
    up_pre = jnp.einsum("prd,pdf->prf", rows, up_weight, preferred_element_type=jnp.float32)
    squash = jax.nn.sigmoid(SWISH_SCALE * gate_pre)
    hidden = (gate_pre * squash * (up_pre + 1.0)).astype(jnp.bfloat16)
    grad_out = jnp.einsum("prd,pfd->prf", upstream, down_weight, preferred_element_type=jnp.float32)
    score = jnp.sum(grad_out * hidden.astype(jnp.float32), axis=2)
    grad_hidden = weight[:, :, None] * grad_out
    slope = squash + SWISH_SCALE * gate_pre * squash * (1.0 - squash)
    grad_pre_gate = (grad_hidden * (up_pre + 1.0) * slope).astype(jnp.bfloat16)
    grad_pre_up = (grad_hidden * gate_pre * squash).astype(jnp.bfloat16)
    scaled_up = (weight[:, :, None] * upstream.astype(jnp.float32)).astype(jnp.bfloat16)
    down_grad = jnp.einsum(
        "prf,prd->pfd", hidden, scaled_up, preferred_element_type=jnp.float32
    ).astype(jnp.bfloat16)
    gate_grad = jnp.einsum(
        "prd,prf->pdf", rows, grad_pre_gate, preferred_element_type=jnp.float32
    ).astype(jnp.bfloat16)
    up_grad = jnp.einsum(
        "prd,prf->pdf", rows, grad_pre_up, preferred_element_type=jnp.float32
    ).astype(jnp.bfloat16)
    back = jnp.einsum(
        "prf,pdf->prd", grad_pre_gate, gate_weight, preferred_element_type=jnp.float32
    )
    back = back + jnp.einsum(
        "prf,pdf->prd", grad_pre_up, up_weight, preferred_element_type=jnp.float32
    )
    return (gate_grad, up_grad, down_grad, back, score)


def body(
    tokens, cotangent, expert_ids, norm_gain, router_weight, gate_weight, up_weight, down_weight
):
    ctx_size = lax.axis_size("ctx")
    local = gate_weight.shape[0]
    experts = router_weight.shape[1]
    rows_here = tokens.shape[0]
    picks = expert_ids.shape[1]
    width = tokens.shape[1]
    assigned = rows_here * picks
    capacity = max(2, rows_here * picks * 5 // (4 * experts))
    slots = experts * capacity
    widened = tokens.astype(jnp.float32)
    inverse = lax.rsqrt(jnp.mean(widened * widened, axis=1, keepdims=True) + EPSILON)
    scaled = widened * inverse
    normed = (scaled * norm_gain).astype(jnp.bfloat16)
    logits = jnp.dot(normed, router_weight, preferred_element_type=jnp.float32)
    labels = jnp.arange(experts, dtype=jnp.int32)
    member = expert_ids[:, :, None] == labels
    chosen = jnp.sum(jnp.where(member, logits[:, None, :], 0.0), axis=2)
    lifted = jnp.exp(chosen)
    gates = lifted / jnp.sum(lifted, axis=1, keepdims=True)
    hits = member.reshape(assigned, experts).astype(jnp.int32)
    rank = jnp.sum((jnp.cumsum(hits, axis=0) - 1) * hits, axis=1)
    position = expert_ids.reshape(-1) * capacity + rank
    match = (jnp.arange(slots, dtype=jnp.int32)[:, None] == position[None, :]).astype(jnp.float32)
    dispatch = jnp.sum(match.reshape(slots, rows_here, picks), axis=2)
    dispatch_low = dispatch.astype(jnp.bfloat16)
    out_rows = jnp.dot(dispatch_low, normed, preferred_element_type=jnp.float32).astype(
        jnp.bfloat16
    )
    out_rows = out_rows.reshape(ctx_size, local, capacity, width)
    out_grad = jnp.dot(dispatch_low, cotangent, preferred_element_type=jnp.float32).astype(
        jnp.bfloat16
    )
    out_grad = out_grad.reshape(ctx_size, local, capacity, width)
    out_gate = jnp.dot(match, gates.reshape(-1), precision=lax.Precision.HIGHEST)
    out_gate = out_gate.reshape(ctx_size, local, capacity)
    arrived = (
        lax.all_to_all(out_rows, "ctx", split_axis=0, concat_axis=2, tiled=True),
        lax.all_to_all(out_grad, "ctx", split_axis=0, concat_axis=2, tiled=True),
        lax.all_to_all(
            out_gate.astype(jnp.bfloat16), "ctx", split_axis=0, concat_axis=2, tiled=True
        ).astype(out_gate.dtype),
    )
    rows, upstream, weight = (
        lax.all_gather(arrived[0], "dp", axis=2, tiled=True),
        lax.all_gather(arrived[1], "dp", axis=2, tiled=True),
        lax.all_gather(arrived[2].astype(jnp.bfloat16), "dp", axis=2, tiled=True).astype(
            jnp.float32
        ),
    )
    gate_grad, up_grad, down_grad, back, score = expert_pass(
        rows[0], upstream[0], weight[0], gate_weight, up_weight, down_weight
    )
    back_mine, score_mine = (
        lax.psum_scatter(back.astype(jnp.bfloat16), "dp", scatter_dimension=1, tiled=True).astype(
            jnp.float32
        ),
        lax.psum_scatter(score.astype(jnp.bfloat16), "dp", scatter_dimension=1, tiled=True).astype(
            jnp.float32
        ),
    )
    back_slots, score_slots = (
        lax.all_to_all(
            back_mine.astype(jnp.bfloat16), "ctx", split_axis=1, concat_axis=0, tiled=True
        ).astype(back_mine.dtype),
        lax.all_to_all(
            score_mine.astype(jnp.bfloat16), "ctx", split_axis=1, concat_axis=0, tiled=True
        ).astype(score_mine.dtype),
    )
    back_flat = back_slots.reshape(slots, width)
    score_flat = score_slots.reshape(slots)
    grad_tok = jnp.dot(dispatch.T, back_flat, precision=lax.Precision.HIGHEST)
    score_tok = jnp.dot(score_flat, match, precision=lax.Precision.HIGHEST).reshape(
        rows_here, picks
    )
    mixed = jnp.sum(gates * score_tok, axis=1, keepdims=True)
    grad_chosen = gates * (score_tok - mixed)
    grad_logits = jnp.sum(jnp.where(member, grad_chosen[:, :, None], 0.0), axis=1).astype(
        jnp.bfloat16
    )
    grad_normed = grad_tok + jnp.dot(
        grad_logits, router_weight.T, preferred_element_type=jnp.float32
    )
    router_part = jnp.dot(normed.T, grad_logits, preferred_element_type=jnp.float32)
    gain_part = jnp.sum(grad_normed * scaled, axis=0)
    router_grad, gain_grad = (
        lax.psum_scatter(router_part, ("dp", "ctx"), scatter_dimension=0, tiled=True),
        lax.psum_scatter(gain_part, ("dp", "ctx"), scatter_dimension=0, tiled=True),
    )
    grad_scaled = grad_normed * norm_gain
    correction = jnp.mean(grad_scaled * scaled, axis=1, keepdims=True)
    grad_input = (
        cotangent.astype(jnp.float32) + inverse * (grad_scaled - scaled * correction)
    ).astype(jnp.bfloat16)
    return (grad_input, gate_grad, up_grad, down_grad, router_grad, gain_grad)


def solution(mesh):
    return jax.shard_map(
        body,
        mesh=mesh,
        in_specs=(
            P(("dp", "ctx"), None),
            P(("dp", "ctx"), None),
            P(("dp", "ctx"), None),
            P(),
            P(),
            P("ctx", None, "dp"),
            P("ctx", None, "dp"),
            P("ctx", "dp", None),
        ),
        out_specs=(
            P(("dp", "ctx"), None),
            P("ctx", None, "dp"),
            P("ctx", None, "dp"),
            P("ctx", "dp", None),
            P(("dp", "ctx"), None),
            P(("dp", "ctx")),
        ),
        check_vma=False,
    )
```

profile of v0, /device:TPU:0, one launch (start us, length us, event | category | flops | bytes accessed | tf_op | source)
XLA Modules:
  0.0 604.0 jit_solution(15963162471281344825)
XLA Ops:
  14.0 59.6 %all_to_all.85 = bf16[8,2,40,1792]{3,2,1,0:T(8,128)(2,1)S(1)} all-to-all(bf16[8,2,40,1792]{3,2,1,0:T(8,128)(2,1)S(1)} %bitcast.98), channel_id=1, replica_groups=mesh['dp'=4,'ctx'=8] {'ctx'}, dimensions={0} | all-to-all | bytes 4587520 | tf_op jit(solution)/shard_map/all_to_all | solution.py:79
  76.0 55.6 %all_to_all.86 = bf16[8,2,40,1792]{3,2,1,0:T(8,128)(2,1)S(1)} all-to-all(bf16[8,2,40,1792]{3,2,1,0:T(8,128)(2,1)S(1)} %bitcast.99), channel_id=1, replica_groups=mesh['dp'=4,'ctx'=8] {'ctx'}, dimensions={0} | all-to-all | bytes 4587520 | tf_op jit(solution)/shard_map/all_to_all | solution.py:80
  137.6 9.5 %fusion.5 = f32[2,1280,384]{1,2,0:T(8,128)} fusion(bf16[2,1792,384]{2,1,0:T(8,128)(2,1)S(1)} %copy-done, bf16[1,2,1280,1792]{3,2,1,0:T(8,128)(2,1)} %all-gather.5.cloned.1.call-done), kind=kOutput, calls=%fused_computation.7 | convolution fusion | flops 3523215360 | bytes 15859712 | tf_op jit(solution)/shard_map/prd,pdf->prf/dot_general | solution.py:11
  147.0 11.1 %fusion.13 = f32[2,1280,384]{1,2,0:T(8,128)} fusion(bf16[2,1792,384]{2,1,0:T(8,128)(2,1)S(1)} %copy-done.6, bf16[1,2,1280,1792]{3,2,1,0:T(8,128)(2,1)} %all-gather.5.cloned.1.call-done), kind=kOutput, calls=%fused_computation.15 | convolution fusion | flops 3524198400 | bytes 15859712 | tf_op jit(solution)/shard_map/prd,pdf->prf/dot_general | solution.py:12
  158.1 43.8 %all-gather.3.cloned.1.call-done = bf16[1,2,1280,1792]{3,2,1,0:T(8,128)(2,1)} async-done(((bf16[1,2,320,1792]{3,2,1,0:T(8,128)(2,1)}), bf16[1,2,1280,1792]{3,2,1,0:T(8,128)(2,1)}) %all-gather.3.cloned.1.call-update) | async-done | bytes 9175056 | tf_op jit(solution)/shard_map/all_gather | solution.py:87
  201.9 13.7 %multiply_reduce_fusion = (bf16[2,1280]{1,0:T(2,128)(2,1)}, bf16[2,1280,384]{1,2,0:T(8,128)(2,1)}, f32[2,1280,384]{1,2,0:T(8,128)}) fusion(f32[2,1280,384]{1,2,0:T(8,128)} %fusion.13, f32[2,1280,384]{1,2,0:T(8,128)} %fusion.5, bf16[2,384,1792]{2,1,0:T(8,128)(2,1)} %param.15, bf16[1,2,1280,1792]{3,2,1,0:T(8,128)(2,1)} %all-gather.3.cloned.1.call-done), kind=kOutput, calls=%fused_computation.16 | convolution fusion | flops 3533043200 | bytes 25695232 | tf_op jit(solution)/shard_map/prd,pfd->prf/dot_general | solution.py:15
  217.9 20.0 %reduce-scatter.8.cloned.1.call-done = bf16[320,2]{1,0:T(8,128)(2,1)} async-done(((bf16[1280,2]{1,0:T(8,128)(2,1)}), bf16[320,2]{1,0:T(8,128)(2,1)}) %reduce-scatter.8.cloned.1.call-update) | async-done | bytes 1296
  239.5 5.5 all-to-all-start.4
  246.1 2.1 eq.110
  248.3 3.3 all-to-all-done.4
  262.0 9.0 %all_to_all.87 = bf16[8,2,40]{2,1,0:T(2,128)(2,1)S(1)} all-to-all(bf16[8,2,40]{2,1,0:T(2,128)(2,1)S(1)} %convert_element_type.83), channel_id=1, replica_groups=mesh['dp'=4,'ctx'=8] {'ctx'}, dimensions={0} | all-to-all | bytes 2560 | tf_op jit(solution)/shard_map/all_to_all | solution.py:81
  274.5 7.1 %all_gather.9 = bf16[1,2,1280]{1,0,2:T(2,128)(2,1)S(1)} all-gather(bf16[1,2,320]{1,0,2:T(2,128)(2,1)} %copy.141), channel_id=1, replica_groups=mesh['dp'=4,'ctx'=8] {'dp'}, dimensions={2}, use_global_device_ids=true | all-gather | bytes 6400 | tf_op jit(solution)/shard_map/all_gather | solution.py:88
  284.9 6.4 %multiply_convert_fusion.3 = (bf16[2,1280,384]{1,2,0:T(8,128)(2,1)}, bf16[2,1280,384]{1,2,0:T(8,128)(2,1)S(1)}) fusion(f32[2,1280,384]{1,2,0:T(8,128)} %fusion.5, f32[2,1280,384]{1,2,0:T(8,128)} %get-tuple-element.14, f32[2,1280]{1,0:T(2,128)} %copy.142, f32[2,1280,384]{1,2,0:T(8,128)} %fusion.13), kind=kLoop, calls=%fused_computation.18 | loop fusion | flops 14745600 | bytes 15738880 | tf_op jit(solution)/shard_map/convert_element_type | solution.py:20
  291.4 9.3 %fusion.52 = f32[2,1280,1792]{2,1,0:T(8,128)} fusion(bf16[2,1280,384]{1,2,0:T(8,128)(2,1)S(1)} %get-tuple-element.13, bf16[2,1792,384]{2,1,0:T(8,128)(2,1)S(1)} %copy-done), kind=kOutput, calls=%fused_computation.77 | convolution fusion | flops 3523215360 | bytes 23068672 | tf_op jit(solution)/shard_map/prf,pdf->prd/dot_general | solution.py:31
  300.7 16.4 %add_convert_fusion = bf16[2,1280,1792]{2,1,0:T(8,128)(2,1)} fusion(f32[2,1280,1792]{2,1,0:T(8,128)} %fusion.52, bf16[2,1280,384]{1,2,0:T(8,128)(2,1)} %get-tuple-element.12, bf16[2,1792,384]{2,1,0:T(8,128)(2,1)} %param.14), kind=kOutput, calls=%fused_computation.1 | convolution fusion | flops 3532390400 | bytes 32243712 | tf_op jit(solution)/shard_map/prf,pdf->prd/dot_general | solution.py:34
  317.2 73.6 %reduce-scatter.6.cloned.1.call-done = bf16[2,320,1792]{2,1,0:T(8,128)(2,1)} async-done(((bf16[2,1280,1792]{2,1,0:T(8,128)(2,1)}), bf16[2,320,1792]{2,1,0:T(8,128)(2,1)}) %reduce-scatter.6.cloned.1.call-update) | async-done | bytes 2293776 | tf_op jit(solution)/shard_map/reduce_scatter | solution.py:96
  390.8 5.4 copy.149
  396.2 5.5 all-to-all-start.3
  403.0 12.0 %fusion.20 = bf16[2,1792,384]{2,1,0:T(8,128)(2,1)} fusion(bf16[2,1280,384]{1,2,0:T(8,128)(2,1)} %get-tuple-element.12, bf16[1,2,1280,1792]{3,2,1,0:T(8,128)(2,1)} %all-gather.5.cloned.1.call-done), kind=kOutput, calls=%fused_computation.23 | convolution fusion | flops 3524591616 | bytes 13893632 | tf_op jit(solution)/shard_map/prd,prf->pdf/dot_general | solution.py:28
  415.0 9.7 %fusion.16 = bf16[2,384,1792]{2,1,0:T(8,128)(2,1)} fusion(bf16[2,1280,384]{1,2,0:T(8,128)(2,1)} %get-tuple-element.11, bf16[1,2,1280,1792]{3,2,1,0:T(8,128)(2,1)} %all-gather.3.cloned.1.call-done, f32[2,1280]{1,0:T(2,128)S(1)} %copy-done.10), kind=kOutput, calls=%fused_computation.21 | convolution fusion | flops 3538354176 | bytes 13903872 | tf_op jit(solution)/shard_map/prf,prd->pfd/dot_general | solution.py:22
  424.7 12.2 %fusion.17 = bf16[2,1792,384]{2,1,0:T(8,128)(2,1)} fusion(bf16[2,1280,384]{1,2,0:T(8,128)(2,1)S(1)} %copy-done.3, bf16[1,2,1280,1792]{3,2,1,0:T(8,128)(2,1)} %all-gather.5.cloned.1.call-done), kind=kOutput, calls=%fused_computation.22 | convolution fusion | flops 3524591616 | bytes 13893632 | tf_op jit(solution)/shard_map/prd,prf->pdf/dot_general | solution.py:25
  436.9 111.6 %all-reduce.4.cloned.1.call-done = f32[1792,16]{0,1:T(8,128)} async-done(((f32[1792,16]{0,1:T(8,128)}), f32[1792,16]{0,1:T(8,128)}) %all-reduce.4.cloned.1.call-update) | async-done | bytes 114704
  553.1 41.1 %all-reduce.1 = f32[1792]{0:T(1024)S(1)} all-reduce(f32[1792]{0:T(1024)S(1)} %get-tuple-element.6), channel_id=5, replica_groups=mesh['dp'=4,'ctx'=8] {'dp','ctx'}, use_global_device_ids=true, to_apply=%region_15.16.clone | all-reduce | flops 1792 | bytes 14336
  594.8 2.5 fusion.34
  (103 shorter events, 43.6 us)
Async XLA Ops:
  7.2 130.4 %copy-start = (bf16[2,1792,384]{2,1,0:T(8,128)(2,1)S(1)}, bf16[2,1792,384]{2,1,0:T(8,128)(2,1)}, u32[]{:S(2)}) copy-start(bf16[2,1792,384]{2,1,0:T(8,128)(2,1)} %param.13) | copy-start | bytes 8257540
  7.2 130.4 %all-gather.5.cloned.1.call-start = ((), (), s32[]{:S(2)}) async-start(), calls=%async_computation.8 | async-start | bytes 11468800 | tf_op jit(solution)/shard_map/all_gather | solution.py:86
  9.6 64.1 %copy-start.16 = (f32[128]{0:T(128)}, f32[128]{0:T(128)S(1)}, u32[]{:S(2)}) copy-start(f32[128]{0:T(128)S(1)} %add_rsqrt_fusion) | copy-start | bytes 1540
  11.1 2.9 copy-start.12
  73.7 1.6 copy-start.7
  75.2 126.7 %all-gather.3.cloned.1.call-start = ((), (), s32[]{:S(2)}) async-start(), calls=%async_computation.7 | async-start | bytes 11468800 | tf_op jit(solution)/shard_map/all_gather | solution.py:87
  131.6 1.9 copy-start.4
  131.6 1.9 copy-start.8
  131.6 3.0 copy-start.11
  133.2 104.7 %reduce-scatter.8.cloned.1.call-start = ((), (), s32[]{:S(2)}) async-start(), calls=%async_computation.10 | async-start | bytes 409600
  137.5 9.5 %copy-start.6 = (bf16[2,1792,384]{2,1,0:T(8,128)(2,1)S(1)}, bf16[2,1792,384]{2,1,0:T(8,128)(2,1)}, u32[]{:S(2)}) copy-start(bf16[2,1792,384]{2,1,0:T(8,128)(2,1)} %param.14) | copy-start | bytes 8257540
  158.1 87.5 %copy-start.14 = (f32[128,4]{0,1:T(4,128)S(1)}, f32[128,4]{0,1:T(4,128)}, u32[]{:S(2)}) copy-start(f32[128,4]{0,1:T(4,128)} %select_reduce_fusion.2) | copy-start | bytes 6148
  239.5 12.0 %all-to-all-start.4 = ((bf16[2,8,40]{2,0,1:T(2,128)(2,1)}), bf16[2,8,40]{2,0,1:T(2,128)(2,1)}, u32[]{:S(2)}, u32[]{:S(2)}) async-start(bf16[2,8,40]{2,0,1:T(2,128)(2,1)} %copy.152), calls=%async_computation.5 | async-start | bytes 8192 | tf_op jit(solution)/shard_map/all_to_all | solution.py:107
  245.0 145.8 %reduce-scatter.6.cloned.1.call-start = ((), (), s32[]{:S(2)}) async-start(), calls=%async_computation.9 | async-start | bytes 11468800 | tf_op jit(solution)/shard_map/reduce_scatter | solution.py:96
  291.4 9.3 %copy-start.2 = (bf16[2,1280,384]{1,2,0:T(8,128)(2,1)}, bf16[2,1280,384]{1,2,0:T(8,128)(2,1)S(1)}, u32[]{:S(2)}) copy-start(bf16[2,1280,384]{1,2,0:T(8,128)(2,1)S(1)} %get-tuple-element.13) | copy-start | bytes 5898244
  317.1 84.8 %copy-start.13 = (f32[128,4]{0,1:T(4,128)S(1)}, f32[128,4]{0,1:T(4,128)}, u32[]{:S(2)}) copy-start(f32[128,4]{0,1:T(4,128)} %get-tuple-element.9) | copy-start | bytes 6148
  317.1 84.8 %copy-start.19 = (f32[128]{0:T(128)S(1)}, f32[128]{0:T(128)}, u32[]{:S(2)}) copy-start(f32[128]{0:T(128)} %get-tuple-element.8) | copy-start | bytes 1540
  317.1 84.9 %copy-start.17 = (f32[128]{0:T(128)S(1)}, f32[128]{0:T(128)}, u32[]{:S(2)}) copy-start(f32[128]{0:T(128)} %copy-done.16) | copy-start | bytes 1540
  396.2 153.7 %all-to-all-start.3 = ((bf16[2,320,1792]{2,0,1:T(2,128)(2,1)}), bf16[2,320,1792]{2,0,1:T(2,128)(2,1)S(1)}, u32[]{:S(2)}, u32[]{:S(2)}) async-start(bf16[2,320,1792]{2,0,1:T(2,128)(2,1)} %copy.149), calls=%async_computation.4 | async-start | bytes 4587520 | tf_op jit(solution)/shard_map/all_to_all | solution.py:104
  401.7 146.8 %all-reduce.4.cloned.1.call-start = ((), (), s32[]{:S(2)}) async-start(), calls=%async_computation.11 | async-start | bytes 229376
  403.0 12.0 %copy-start.10 = (f32[2,1280]{1,0:T(2,128)S(1)}, f32[2,1280]{1,0:T(2,128)}, u32[]{:S(2)}) copy-start(f32[2,1280]{1,0:T(2,128)} %copy.142) | copy-start | bytes 30724
  415.0 9.7 %copy-start.3 = (bf16[2,1280,384]{1,2,0:T(8,128)(2,1)S(1)}, bf16[2,1280,384]{1,2,0:T(8,128)(2,1)}, u32[]{:S(2)}) copy-start(bf16[2,1280,384]{1,2,0:T(8,128)(2,1)} %copy-done.2) | copy-start | bytes 5898244
  550.1 1.6 copy-start.5
  550.3 46.9 %copy-start.1 = (bf16[2,1792,384]{2,1,0:T(8,128)(2,1)S(1)}, bf16[2,1792,384]{2,1,0:T(8,128)(2,1)}, u32[]{:S(2)}) copy-start(bf16[2,1792,384]{2,1,0:T(8,128)(2,1)} %param.13) | copy-start | bytes 8257540
  (3 other events, 3.7 us)
Sparse Core Ops, SparseCore 0:
  75.3 61.6 all-gather.4
  139.2 62.7 all-gather.2
  217.4 20.4 reduce-scatter.7
  317.2 73.4 reduce-scatter.5
  408.3 140.1 all-reduce.3
where the time goes:
time: 608 us; the launch traced here: 604 us
  waiting for transfers between devices  252 us (41%)
  blocking collectives  172 us (28%)
  matrix products  103 us (17%)
  local copies, waits for them, and re-layouts  28.2 us (5%)
  other arithmetic  21.1 us (3%)
  between operations  14.4 us (2%)
  starting transfers between devices  12.3 us (2%)
    unnamed x7, waiting for transfers between devices  132 us
    reduce_scatter x1, waiting for transfers between devices, body(): lax.psum_scatter(back.astype(jnp.bfloat16), 'dp', scatter_dimension=1, ti...  73.6 us
    all_to_all x1, blocking collectives, body(): lax.all_to_all(out_rows, 'ctx', split_axis=0, concat_axis=2, tiled=True)  59.6 us
    all_to_all x1, blocking collectives, body(): lax.all_to_all(out_grad, 'ctx', split_axis=0, concat_axis=2, tiled=True)  55.6 us
    all_gather x1, waiting for transfers between devices, body(): lax.all_gather(arrived[1], 'dp', axis=2, tiled=True)  43.8 us
    unnamed x1, blocking collectives  41.1 us
    dot_general x1, matrix products, expert_pass(): jnp.einsum('prf,pdf->prd', grad_pre_up, up_weight, preferred_element_type...  16.4 us
    dot_general x1, matrix products, expert_pass(): jnp.einsum('prd,pfd->prf', upstream, down_weight, preferred_element_type=...  13.7 us
  transfers between devices with their start and end apart: 7, of which 5 were waited for; matrix products, arithmetic and copies ran while one was open for 11% of the time, Pallas kernels for 0%

commit v1 on v0

--- a/solution.py
+++ b/solution.py
@@ -1,10 +1,343 @@
+import functools
+
 import jax
 import jax.numpy as jnp
 from jax import lax
+from jax.experimental import pallas as pl
+from jax.experimental.pallas import tpu as pltpu
 from jax.sharding import PartitionSpec as P
 
 EPSILON = 1e-05
 SWISH_SCALE = 1.702
+MESH = pl.DeviceIdType.MESH
+ANY = pl.BlockSpec(memory_space=pl.ANY)
+VMEM = pl.BlockSpec(memory_space=pltpu.VMEM)
+
+
+def greet_all(n_dp, n_ctx):
+    n = n_dp * n_ctx
+    me = lax.axis_index("dp") * n_ctx + lax.axis_index("ctx")
+    barrier = pltpu.get_barrier_semaphore()
+
+    def hello(i, carry):
+        peer = lax.rem(me + i, n)
+        pl.semaphore_signal(
+            barrier,
+            inc=1,
+            device_id=(lax.div(peer, n_ctx), lax.rem(peer, n_ctx)),
+            device_id_type=MESH,
+        )
+        return carry
+
+    lax.fori_loop(1, n, hello, 0)
+    pl.semaphore_wait(barrier, n - 1)
+
+
+def spread_copy(n_dp, n_ctx, i, src_of, land, send_sem, recv_sem, sending):
+    n = n_dp * n_ctx
+    me = lax.axis_index("dp") * n_ctx + lax.axis_index("ctx")
+    peer = lax.rem(me + i, n)
+    source = me if sending else lax.rem(me + n - i, n)
+    return pltpu.make_async_remote_copy(
+        src_ref=src_of(peer),
+        dst_ref=land.at[source],
+        send_sem=send_sem.at[i],
+        recv_sem=recv_sem.at[i],
+        device_id=(lax.div(peer, n_ctx), lax.rem(peer, n_ctx)),
+        device_id_type=MESH,
+    )
+
+
+def exchange_kernel(n_dp, n_ctx, keep, x_ref, o_ref, land, send_sem, recv_sem):
+    n = n_dp * n_ctx
+    me = lax.axis_index("dp") * n_ctx + lax.axis_index("ctx")
+    greet_all(n_dp, n_ctx)
+    src_of = lambda peer: x_ref.at[peer]
+
+    def start(i, carry):
+        spread_copy(n_dp, n_ctx, i, src_of, land, send_sem, recv_sem, True).start()
+        return carry
+
+    lax.fori_loop(1, n, start, 0)
+    land[pl.ds(me, 1)] = x_ref[pl.ds(me, 1)]
+
+    def finish(i, carry):
+        spread_copy(n_dp, n_ctx, i, src_of, land, send_sem, recv_sem, True).wait_send()
+        spread_copy(n_dp, n_ctx, i, src_of, land, send_sem, recv_sem, False).wait_recv()
+        return carry
+
+    lax.fori_loop(1, n, finish, 0)
+    o_ref[...] = jnp.sum(land[...].reshape(n // keep, keep, 8, 128), axis=0)
+
+
+def exchange(x, n_dp, n_ctx, keep, cid):
+    n = n_dp * n_ctx
+    return pl.pallas_call(
+        functools.partial(exchange_kernel, n_dp, n_ctx, keep),
+        out_shape=jax.ShapeDtypeStruct((keep, 8, 128), jnp.float32),
+        in_specs=[VMEM],
+        out_specs=VMEM,
+        scratch_shapes=[
+            pltpu.VMEM((n, 8, 128), jnp.float32),
+            pltpu.SemaphoreType.DMA((n,)),
+            pltpu.SemaphoreType.DMA((n,)),
+        ],
+        compiler_params=pltpu.CompilerParams(collective_id=cid, has_side_effects=True),
+    )(x)
+
+
+def dispatch_kernel(
+    n_dp, n_ctx, rows_ref, grad_ref, gate_ref, out_rows, out_grad, out_gate,
+    own, own_sem, gate_send, gate_recv, ring_send, ring_recv, far_send, far_recv, sib_send, sib_recv,
+):
+    n = n_dp * n_ctx
+    d, c = lax.axis_index("dp"), lax.axis_index("ctx")
+    me = d * n_ctx + c
+    far = lax.rem(d + 2, n_dp)
+    sib = d + 1 - 2 * lax.rem(d, 2)
+    far_sib = lax.rem(sib + 2, n_dp)
+    greet_all(n_dp, n_ctx)
+    gate_src = lambda peer: gate_ref.at[lax.rem(peer, n_ctx)]
+    ins, outs = (rows_ref, grad_ref), (out_rows, out_grad)
+
+    def gate_start(i, carry):
+        spread_copy(n_dp, n_ctx, i, gate_src, out_gate, gate_send, gate_recv, True).start()
+        return carry
+
+    lax.fori_loop(1, n, gate_start, 0)
+
+    def ring(a, k, sending):
+        peer = lax.rem(c + k, n_ctx)
+        owner = c if sending else lax.rem(c + n_ctx - k, n_ctx)
+        return pltpu.make_async_remote_copy(
+            src_ref=ins[a].at[peer],
+            dst_ref=outs[a].at[:, d * n_ctx + owner],
+            send_sem=ring_send.at[a, k],
+            recv_sem=ring_recv.at[a, k],
+            device_id=(d, peer),
+            device_id_type=MESH,
+        )
+
+    def forward(a, k, src, slot, to, send_sem, recv_sem, index):
+        return pltpu.make_async_remote_copy(
+            src_ref=src,
+            dst_ref=outs[a].at[:, slot],
+            send_sem=send_sem.at[a, index],
+            recv_sem=recv_sem.at[a, index],
+            device_id=(to, c),
+            device_id_type=MESH,
+        )
+
+    def held(a, row, k):
+        owner = lax.rem(c + n_ctx - k, n_ctx)
+        slot = row * n_ctx + owner
+        return slot, (outs[a].at[:, slot])
+
+    loads = []
+    for a in range(2):
+        load = pltpu.make_async_copy(ins[a].at[c], own.at[a], own_sem.at[a])
+        load.start()
+        loads.append(load)
+        for k in range(1, n_ctx):
+            ring(a, k, True).start()
+    stores = []
+    for a in range(2):
+        loads[a].wait()
+        store = pltpu.make_async_copy(own.at[a], outs[a].at[:, me], own_sem.at[a])
+        store.start()
+        stores.append(store)
+    out_gate[pl.ds(me, 1)] = gate_ref[pl.ds(c, 1)]
+
+    def pass_far(a, k, wait):
+        slot, here = held(a, d, k)
+        src = ins[a].at[c] if k == 0 else here
+        for copy in (
+            forward(a, k, src, slot, far, far_send, far_recv, k),
+            forward(a, k, src, slot, sib, sib_send, sib_recv, k),
+        ):
+            copy.wait_send() if wait else copy.start()
+
+    def pass_sib(a, k, wait):
+        slot, here = held(a, far, k)
+        copy = forward(a, k, here, slot, sib, sib_send, sib_recv, n_ctx + k)
+        copy.wait_send() if wait else copy.start()
+
+    def await_far(a, k):
+        slot, here = held(a, far, k)
+        forward(a, k, here, slot, far, far_send, far_recv, k).wait_recv()
+
+    lag = 2
+    for step in range(2 * n_ctx + lag):
+        a, k = divmod(step, n_ctx)
+        if step < 2 * n_ctx:
+            if k > 0:
+                ring(a, k, False).wait_recv()
+            pass_far(a, k, False)
+        if step >= lag:
+            a, k = divmod(step - lag, n_ctx)
+            await_far(a, k)
+            pass_sib(a, k, False)
+    for a in range(2):
+        for k in range(n_ctx):
+            slot, here = held(a, sib, k)
+            forward(a, k, here, slot, sib, sib_send, sib_recv, k).wait_recv()
+            slot, here = held(a, far_sib, k)
+            forward(a, k, here, slot, sib, sib_send, sib_recv, n_ctx + k).wait_recv()
+    for a in range(2):
+        stores[a].wait()
+        for k in range(n_ctx):
+            if k > 0:
+                ring(a, k, True).wait_send()
+            pass_far(a, k, True)
+            pass_sib(a, k, True)
+
+    def gate_finish(i, carry):
+        spread_copy(n_dp, n_ctx, i, gate_src, out_gate, gate_send, gate_recv, True).wait_send()
+        spread_copy(n_dp, n_ctx, i, gate_src, out_gate, gate_send, gate_recv, False).wait_recv()
+        return carry
+
+    lax.fori_loop(1, n, gate_finish, 0)
+
+
+def dispatch_rows(rows, grad, gate, n_dp, n_ctx):
+    n = n_dp * n_ctx
+    _, local, cap, width = rows.shape
+    arrived = jax.ShapeDtypeStruct((local, n, cap, width), rows.dtype)
+    return pl.pallas_call(
+        functools.partial(dispatch_kernel, n_dp, n_ctx),
+        out_shape=(arrived, arrived, jax.ShapeDtypeStruct((n, 8, 128), jnp.float32)),
+        in_specs=[ANY, ANY, VMEM],
+        out_specs=(ANY, ANY, VMEM),
+        scratch_shapes=[
+            pltpu.VMEM((2, local, cap, width), rows.dtype),
+            pltpu.SemaphoreType.DMA((2,)),
+            pltpu.SemaphoreType.DMA((n,)),
+            pltpu.SemaphoreType.DMA((n,)),
+            pltpu.SemaphoreType.DMA((2, n_ctx)),
+            pltpu.SemaphoreType.DMA((2, n_ctx)),
+            pltpu.SemaphoreType.DMA((2, n_ctx)),
+            pltpu.SemaphoreType.DMA((2, n_ctx)),
+            pltpu.SemaphoreType.DMA((2, 2 * n_ctx)),
+            pltpu.SemaphoreType.DMA((2, 2 * n_ctx)),
+        ],
+        compiler_params=pltpu.CompilerParams(collective_id=0, has_side_effects=True),
+    )(rows, grad, gate)
+
+
+def return_kernel(
+    n_dp, n_ctx, back_ref, out_ref,
+    mine, sib_land, far_out, far_land, done,
+    mine_sem, sib_send, sib_recv, far_send, far_recv, ring_send, ring_recv, own_sem,
+):
+    d, c = lax.axis_index("dp"), lax.axis_index("ctx")
+    far = lax.rem(d + 2, n_dp)
+    sib = d + 1 - 2 * lax.rem(d, 2)
+    far_sib = lax.rem(sib + 2, n_dp)
+    greet_all(n_dp, n_ctx)
+
+    def dest(k):
+        return lax.rem(c + k, n_ctx)
+
+    def to_sib(k, which):
+        row = far_sib if which == 0 else sib
+        return pltpu.make_async_remote_copy(
+            src_ref=back_ref.at[:, row * n_ctx + dest(k)],
+            dst_ref=sib_land.at[k, which],
+            send_sem=sib_send.at[k, which],
+            recv_sem=sib_recv.at[k, which],
+            device_id=(sib, c),
+            device_id_type=MESH,
+        )
+
+    def load(k, which):
+        row = far if which == 0 else d
+        return pltpu.make_async_copy(
+            back_ref.at[:, row * n_ctx + dest(k)], mine.at[k, which], mine_sem.at[k, which]
+        )
+
+    def to_far(k):
+        return pltpu.make_async_remote_copy(
+            src_ref=far_out.at[k],
+            dst_ref=far_land.at[k],
+            send_sem=far_send.at[k],
+            recv_sem=far_recv.at[k],
+            device_id=(far, c),
+            device_id_type=MESH,
+        )
+
+    def ring(k, sending):
+        owner = c if sending else lax.rem(c + n_ctx - k, n_ctx)
+        return pltpu.make_async_remote_copy(
+            src_ref=done.at[k],
+            dst_ref=out_ref.at[owner],
+            send_sem=ring_send.at[k],
+            recv_sem=ring_recv.at[k],
+            device_id=(d, dest(k)),
+            device_id_type=MESH,
+        )
+
+    order = list(range(1, n_ctx)) + [0]
+    for k in order:
+        for which in range(2):
+            to_sib(k, which).start()
+            load(k, which).start()
+    for k in order:
+        to_sib(k, 0).wait_recv()
+        load(k, 0).wait()
+        far_out[k] = (
+            mine[k, 0].astype(jnp.float32) + sib_land[k, 0].astype(jnp.float32)
+        ).astype(jnp.bfloat16)
+        to_far(k).start()
+    for k in order:
+        to_sib(k, 1).wait_recv()
+        load(k, 1).wait()
+        to_far(k).wait_recv()
+        done[k] = (
+            mine[k, 1].astype(jnp.float32)
+            + sib_land[k, 1].astype(jnp.float32)
+            + far_land[k].astype(jnp.float32)
+        ).astype(jnp.bfloat16)
+        if k > 0:
+            ring(k, True).start()
+    own = pltpu.make_async_copy(done.at[0], out_ref.at[c], own_sem)
+    own.start()
+    own.wait()
+    for k in order:
+        to_sib(k, 0).wait_send()
+        to_sib(k, 1).wait_send()
+        to_far(k).wait_send()
+        if k > 0:
+            ring(k, True).wait_send()
+            ring(k, False).wait_recv()
+
+
+def return_rows(back, n_dp, n_ctx):
+    local, n, cap, width = back.shape
+    block = (local, cap, width)
+    return pl.pallas_call(
+        functools.partial(return_kernel, n_dp, n_ctx),
+        out_shape=jax.ShapeDtypeStruct((n_ctx,) + block, back.dtype),
+        in_specs=[ANY],
+        out_specs=ANY,
+        scratch_shapes=[
+            pltpu.VMEM((n_ctx, 2) + block, back.dtype),
+            pltpu.VMEM((n_ctx, 2) + block, back.dtype),
+            pltpu.VMEM((n_ctx,) + block, back.dtype),
+            pltpu.VMEM((n_ctx,) + block, back.dtype),
+            pltpu.VMEM((n_ctx,) + block, back.dtype),
+            pltpu.SemaphoreType.DMA((n_ctx, 2)),
+            pltpu.SemaphoreType.DMA((n_ctx, 2)),
+            pltpu.SemaphoreType.DMA((n_ctx, 2)),
+            pltpu.SemaphoreType.DMA((n_ctx,)),
+            pltpu.SemaphoreType.DMA((n_ctx,)),
+            pltpu.SemaphoreType.DMA((n_ctx,)),
+            pltpu.SemaphoreType.DMA((n_ctx,)),
+            pltpu.SemaphoreType.DMA,
+        ],
+        compiler_params=pltpu.CompilerParams(
+            collective_id=1, has_side_effects=True, vmem_limit_bytes=48 * 1024 * 1024
+        ),
+    )(back)
 
 
 def expert_pass(rows, upstream, weight, gate_weight, up_weight, down_weight):
@@ -37,10 +370,16 @@
     return (gate_grad, up_grad, down_grad, back, score)
 
 
+def tiles(x):
+    return jnp.pad(x, ((0, 0), (0, 1024 - x.shape[1]))).reshape(x.shape[0], 8, 128)
+
+
 def body(
     tokens, cotangent, expert_ids, norm_gain, router_weight, gate_weight, up_weight, down_weight
 ):
-    ctx_size = lax.axis_size("ctx")
+    n_ctx = lax.axis_size("ctx")
+    n_dp = lax.axis_size("dp")
+    n = n_dp * n_ctx
     local = gate_weight.shape[0]
     experts = router_weight.shape[1]
     rows_here = tokens.shape[0]
@@ -48,6 +387,7 @@
     width = tokens.shape[1]
     assigned = rows_here * picks
     capacity = max(2, rows_here * picks * 5 // (4 * experts))
+    capacity = -(-capacity // 8) * 8
     slots = experts * capacity
     widened = tokens.astype(jnp.float32)
     inverse = lax.rsqrt(jnp.mean(widened * widened, axis=1, keepdims=True) + EPSILON)
@@ -68,49 +408,29 @@
     out_rows = jnp.dot(dispatch_low, normed, preferred_element_type=jnp.float32).astype(
         jnp.bfloat16
     )
-    out_rows = out_rows.reshape(ctx_size, local, capacity, width)
+    out_rows = out_rows.reshape(n_ctx, local, capacity, width)
     out_grad = jnp.dot(dispatch_low, cotangent, preferred_element_type=jnp.float32).astype(
         jnp.bfloat16
     )
-    out_grad = out_grad.reshape(ctx_size, local, capacity, width)
+    out_grad = out_grad.reshape(n_ctx, local, capacity, width)
     out_gate = jnp.dot(match, gates.reshape(-1), precision=lax.Precision.HIGHEST)
-    out_gate = out_gate.reshape(ctx_size, local, capacity)
-    arrived = (
-        lax.all_to_all(out_rows, "ctx", split_axis=0, concat_axis=2, tiled=True),
-        lax.all_to_all(out_grad, "ctx", split_axis=0, concat_axis=2, tiled=True),
-        lax.all_to_all(
-            out_gate.astype(jnp.bfloat16), "ctx", split_axis=0, concat_axis=2, tiled=True
-        ).astype(out_gate.dtype),
-    )
-    rows, upstream, weight = (
-        lax.all_gather(arrived[0], "dp", axis=2, tiled=True),
-        lax.all_gather(arrived[1], "dp", axis=2, tiled=True),
-        lax.all_gather(arrived[2].astype(jnp.bfloat16), "dp", axis=2, tiled=True).astype(
-            jnp.float32
-        ),
-    )
+    out_gate = tiles(out_gate.reshape(n_ctx, local * capacity))
+    rows, upstream, weight = dispatch_rows(out_rows, out_grad, out_gate, n_dp, n_ctx)
+    rows = rows.reshape(local, n * capacity, width)
+    upstream = upstream.reshape(local, n * capacity, width)
+    weight = weight.reshape(n, 1024)[:, : local * capacity].reshape(n, local, capacity)
+    weight = weight.transpose(1, 0, 2).reshape(local, n * capacity)
     gate_grad, up_grad, down_grad, back, score = expert_pass(
-        rows[0], upstream[0], weight[0], gate_weight, up_weight, down_weight
-    )
-    back_mine, score_mine = (
-        lax.psum_scatter(back.astype(jnp.bfloat16), "dp", scatter_dimension=1, tiled=True).astype(
-            jnp.float32
-        ),
-        lax.psum_scatter(score.astype(jnp.bfloat16), "dp", scatter_dimension=1, tiled=True).astype(
-            jnp.float32
-        ),
-    )
-    back_slots, score_slots = (
-        lax.all_to_all(
-            back_mine.astype(jnp.bfloat16), "ctx", split_axis=1, concat_axis=0, tiled=True
-        ).astype(back_mine.dtype),
-        lax.all_to_all(
-            score_mine.astype(jnp.bfloat16), "ctx", split_axis=1, concat_axis=0, tiled=True
-        ).astype(score_mine.dtype),
+        rows, upstream, weight, gate_weight, up_weight, down_weight
+    )
+    score_out = score.reshape(local, n, capacity).transpose(1, 0, 2).reshape(n, local * capacity)
+    score_slots = exchange(tiles(score_out), n_dp, n_ctx, n_ctx, 2)
+    back_slots = return_rows(
+        back.astype(jnp.bfloat16).reshape(local, n, capacity, width), n_dp, n_ctx
     )
     back_flat = back_slots.reshape(slots, width)
-    score_flat = score_slots.reshape(slots)
-    grad_tok = jnp.dot(dispatch.T, back_flat, precision=lax.Precision.HIGHEST)
+    score_flat = score_slots.reshape(n_ctx, 1024)[:, : local * capacity].reshape(slots)
+    grad_tok = jnp.dot(dispatch_low.T, back_flat, preferred_element_type=jnp.float32)
     score_tok = jnp.dot(score_flat, match, precision=lax.Precision.HIGHEST).reshape(
         rows_here, picks
     )
@@ -124,10 +444,13 @@
     )
     router_part = jnp.dot(normed.T, grad_logits, preferred_element_type=jnp.float32)
     gain_part = jnp.sum(grad_normed * scaled, axis=0)
-    router_grad, gain_grad = (
-        lax.psum_scatter(router_part, ("dp", "ctx"), scatter_dimension=0, tiled=True),
-        lax.psum_scatter(gain_part, ("dp", "ctx"), scatter_dimension=0, tiled=True),
-    )
+    share = width // n
+    parts = jnp.concatenate(
+        [router_part.reshape(n, share * experts), gain_part.reshape(n, share)], axis=1
+    )
+    sums = exchange(tiles(parts), n_dp, n_ctx, 1, 3).reshape(1024)
+    router_grad = sums[: share * experts].reshape(share, experts)
+    gain_grad = sums[share * experts : share * experts + share]
     grad_scaled = grad_normed * norm_gain
     correction = jnp.mean(grad_scaled * scaled, axis=1, keepdims=True)
     grad_input = (

time: 608 us -> 383 us (0.63)
  waiting for transfers between devices: 252 us -> 0 us
  Pallas kernels: 0 us -> 244 us
  blocking collectives: 172 us -> 0 us
  local copies, waits for them, and re-layouts: 28.2 us -> 12.1 us
  other arithmetic: 21.1 us -> 7.95 us
  between operations: 14.4 us -> 1.33 us
  starting transfers between devices: 12.3 us -> 0 us
  matrix products: 103 us -> 114 us
    pallas_call x0 -> x4, Pallas kernels: none -> 244 us  [the longest x1 129 us: dispatch_rows(): pl.pallas_call(functools.partial(dispatch_kernel, n_dp, n_ctx), out_shape...]
    unnamed x7 -> x0, waiting for transfers between devices: 132 us -> none
    all_to_all x3 -> x0, blocking collectives: 124 us -> none  [the longest x1 59.6 us: body(): lax.all_to_all(out_rows, 'ctx', split_axis=0, concat_axis=2, tiled=True)]
    reduce_scatter x1 -> x0, waiting for transfers between devices: 73.6 us -> none  [body(): lax.psum_scatter(back.astype(jnp.bfloat16), 'dp', scatter_dimension=1, ti...]
    all_gather x2 -> x0, waiting for transfers between devices: 43.8 us -> none  [the longest x1 43.8 us: body(): lax.all_gather(arrived[1], 'dp', axis=2, tiled=True)]
    unnamed x1 -> x0, blocking collectives: 41.1 us -> none
    all_to_all x2 -> x0, starting transfers between devices: 11 us -> none  [the longest x1 5.52 us: body(): lax.all_to_all(back_mine.astype(jnp.bfloat16), 'ctx', split_axis=1, conca...]
    dot_general x1, matrix products: 13.7 us -> 24.2 us  [expert_pass(): jnp.einsum('prd,pfd->prf', upstream, down_weight, preferred_element_type=...]
  transfers between devices with their start and end apart: 7 -> 0, of which waited for: 5 -> 0; matrix products, arithmetic and copies ran while one was open for 11% -> 0% of each run, Pallas kernels for 0% -> 0%
where the time goes in v1:
time: 383 us; the launch traced here: 380 us
  Pallas kernels  244 us (64%)
  matrix products  114 us (30%)
  local copies, waits for them, and re-layouts  12.1 us (3%)
  other arithmetic  7.95 us (2%)
    pallas_call x1, Pallas kernels, dispatch_rows(): pl.pallas_call(functools.partial(dispatch_kernel, n_dp, n_ctx), out_shape...  129 us
    pallas_call x1, Pallas kernels, return_rows(): pl.pallas_call(functools.partial(return_kernel, n_dp, n_ctx), out_shape=j...  65.2 us
    pallas_call x2, Pallas kernels, exchange(): pl.pallas_call(functools.partial(exchange_kernel, n_dp, n_ctx, keep), out...  50.5 us
    dot_general x1, matrix products, expert_pass(): jnp.einsum('prd,pfd->prf', upstream, down_weight, preferred_element_type=...  24.2 us
    dot_general x1, matrix products, expert_pass(): jnp.einsum('prf,pdf->prd', grad_pre_up, up_weight, preferred_element_type...  16.4 us
    dot_general x1, matrix products, expert_pass(): jnp.einsum('prd,prf->pdf', rows, grad_pre_up, preferred_element_type=jnp....  12.2 us
    dot_general x1, matrix products, expert_pass(): jnp.einsum('prd,prf->pdf', rows, grad_pre_gate, preferred_element_type=jn...  12 us
    dot_general x1, matrix products, expert_pass(): jnp.einsum('prf,pdf->prd', grad_pre_gate, gate_weight, preferred_element_...  11.3 us

profile of v1, /device:TPU:0, one launch (start us, length us, event | category | flops | bytes accessed | tf_op | source)
XLA Modules:
  0.0 379.7 jit_solution(6552514881417987937)
XLA Ops:
  0.7 1.3 fusion.16
  2.0 1.3 fusion.31
  5.4 1.2 reduce-window.6
  9.4 1.0 iota_compare_fusion
  10.4 2.1 eq.101
  12.5 3.1 convolution_convert_fusion.2
  15.7 2.2 convolution_convert_fusion.3
  17.9 128.6 %shard_map.127 = (bf16[2,32,40,1792]{3,2,1,0:T(8,128)(2,1)}, bf16[2,32,40,1792]{3,2,1,0:T(8,128)(2,1)}, f32[32,8,128]{2,1,0:T(8,128)}) custom-call(bf16[8,2,40,1792]{3,2,1,0:T(8,128)(2,1)} %bitcast.76, bf16[8,2,40,1792]{3,2,1,0:T(8,128)(2,1)} %bitcast.75, f32[8,8,128]{2,1,0:T(8,128)} %bitcast.80), custom_call_target="tpu_custom_call" | custom-call | tf_op jit(solution)/shard_map/pallas_call | solution.py:206
  147.6 9.5 %fusion.34 = f32[2,1280,384]{1,2,0:T(8,128)} fusion(bf16[2,1280,1792]{2,1,0:T(8,128)(2,1)} %bitcast.89, bf16[2,1792,384]{2,1,0:T(8,128)(2,1)S(1)} %copy-done), kind=kOutput, calls=%fused_computation.74 | convolution fusion | flops 3523215360 | bytes 15859712 | tf_op jit(solution)/shard_map/prd,pdf->prf/dot_general | solution.py:344
  157.2 9.5 %convolution_add_fusion = f32[2,1280,384]{1,2,0:T(8,128)} fusion(bf16[2,1280,1792]{2,1,0:T(8,128)(2,1)} %bitcast.90, bf16[2,1792,384]{2,1,0:T(8,128)(2,1)S(1)} %copy-done.2), kind=kOutput, calls=%fused_computation.9 | convolution fusion | flops 3524198400 | bytes 15859712 | tf_op jit(solution)/shard_map/prd,pdf->prf/dot_general | solution.py:345
  166.6 24.2 %multiply_reduce_fusion = (f32[2,1280]{1,0:T(2,128)S(1)}, bf16[2,1280,384]{1,2,0:T(8,128)(2,1)S(1)}, bf16[2,1280,384]{1,2,0:T(8,128)(2,1)}, bf16[2,1280,384]{1,2,0:T(8,128)(2,1)}) fusion(f32[2,1280,384]{1,2,0:T(8,128)} %convolution_add_fusion, f32[2,1280,384]{1,2,0:T(8,128)} %fusion.34, f32[2,1280]{1,0:T(2,128)S(1)} %mul.128, ...), kind=kOutput, calls=%fused_computation.4 | convolution fusion | flops 3543856640 | bytes 25710592 | tf_op jit(solution)/shard_map/prd,pfd->prf/dot_general | solution.py:348
  190.8 9.1 %fusion.2 = bf16[2,384,1792]{2,1,0:T(8,128)(2,1)} fusion(bf16[2,1280,384]{1,2,0:T(8,128)(2,1)S(1)} %get-tuple-element.45, bf16[2,1280,1792]{2,1,0:T(8,128)(2,1)} %bitcast.94, f32[2,1280]{1,0:T(2,128)S(1)} %mul.128), kind=kOutput, calls=%fused_computation.10 | convolution fusion | flops 3538354176 | bytes 13903872 | tf_op jit(solution)/shard_map/prf,prd->pfd/dot_general | solution.py:355
  200.8 34.5 %shard_map.129 = f32[8,8,128]{2,1,0:T(8,128)} custom-call(f32[32,8,128]{2,1,0:T(8,128)} %bitcast.77), custom_call_target="tpu_custom_call" | custom-call | tf_op jit(solution)/shard_map/pallas_call | solution.py:75
  236.2 1.5 select_reduce_fusion
  237.8 1.3 fusion.23
  239.1 1.5 reshape.196
  240.6 12.0 %convolution_convert_fusion.1 = bf16[2,1792,384]{2,1,0:T(8,128)(2,1)} fusion(bf16[2,1280,1792]{2,1,0:T(8,128)(2,1)} %bitcast.91, bf16[2,1280,384]{1,2,0:T(8,128)(2,1)} %get-tuple-element.46), kind=kOutput, calls=%fused_computation.12 | convolution fusion | flops 3524591616 | bytes 13893632 | tf_op jit(solution)/shard_map/prd,prf->pdf/dot_general | solution.py:358
  252.5 12.2 %convolution_convert_fusion = bf16[2,1792,384]{2,1,0:T(8,128)(2,1)} fusion(bf16[2,1280,1792]{2,1,0:T(8,128)(2,1)} %bitcast.92, bf16[2,1280,384]{1,2,0:T(8,128)(2,1)} %get-tuple-element.47), kind=kOutput, calls=%fused_computation.11 | convolution fusion | flops 3524591616 | bytes 13893632 | tf_op jit(solution)/shard_map/prd,prf->pdf/dot_general | solution.py:361
  264.7 11.3 %fusion.35 = f32[2,1280,1792]{2,1,0:T(8,128)} fusion(bf16[2,1280,384]{1,2,0:T(8,128)(2,1)} %get-tuple-element.46, bf16[2,1792,384]{2,1,0:T(8,128)(2,1)S(1)} %copy-done), kind=kOutput, calls=%fused_computation.75 | convolution fusion | flops 3523215360 | bytes 23068672 | tf_op jit(solution)/shard_map/prf,pdf->prd/dot_general | solution.py:364
  276.0 16.4 %add_convert_fusion = bf16[2,1280,1792]{2,1,0:T(8,128)(2,1)} fusion(f32[2,1280,1792]{2,1,0:T(8,128)} %fusion.35, bf16[2,1280,384]{1,2,0:T(8,128)(2,1)} %get-tuple-element.47, bf16[2,1792,384]{2,1,0:T(8,128)(2,1)} %param.14), kind=kOutput, calls=%fused_computation.1 | convolution fusion | flops 3532390400 | bytes 32243712 | tf_op jit(solution)/shard_map/prf,pdf->prd/dot_general | solution.py:367
  292.4 65.2 %shard_map.128 = bf16[8,2,40,1792]{3,2,1,0:T(8,128)(2,1)S(1)} custom-call(bf16[2,32,40,1792]{3,2,1,0:T(8,128)(2,1)} %bitcast.74), custom_call_target="tpu_custom_call" | custom-call | tf_op jit(solution)/shard_map/pallas_call | solution.py:317
  358.7 1.1 fusion.14
  360.6 16.0 %shard_map.130 = f32[1,8,128]{2,1,0:T(8,128)} custom-call(f32[32,8,128]{2,1,0:T(8,128)} %bitcast.78), custom_call_target="tpu_custom_call" | custom-call | tf_op jit(solution)/shard_map/pallas_call | solution.py:75
  376.6 1.2 slice.24
  (62 shorter events, 11.1 us)
Async XLA Ops:
  0.6 147.0 %copy-start = (bf16[2,1792,384]{2,1,0:T(8,128)(2,1)S(1)}, bf16[2,1792,384]{2,1,0:T(8,128)(2,1)}, u32[]{:S(2)}) copy-start(bf16[2,1792,384]{2,1,0:T(8,128)(2,1)} %param.13) | copy-start | bytes 8257540
  0.6 15.0 %copy-start.1 = (bf16[128,1792]{1,0:T(8,128)(2,1)S(1)}, bf16[128,1792]{1,0:T(8,128)(2,1)}, u32[]{:S(2)}) copy-start(bf16[128,1792]{1,0:T(8,128)(2,1)} %param.8) | copy-start | bytes 1376260
  0.7 15.0 %copy-start.4 = (f32[1792]{0:T(1024)S(1)}, f32[1792]{0:T(1024)}, u32[]{:S(2)}) copy-start(f32[1792]{0:T(1024)} %param.11) | copy-start | bytes 21508
  147.6 9.5 %copy-start.2 = (bf16[2,1792,384]{2,1,0:T(8,128)(2,1)S(1)}, bf16[2,1792,384]{2,1,0:T(8,128)(2,1)}, u32[]{:S(2)}) copy-start(bf16[2,1792,384]{2,1,0:T(8,128)(2,1)} %param.14) | copy-start | bytes 8257540
  190.8 46.9 %copy-start.6 = (s32[128,4]{0,1:T(4,128)S(1)}, s32[128,4]{0,1:T(4,128)}, u32[]{:S(2)}) copy-start(s32[128,4]{0,1:T(4,128)} %param.10) | copy-start | bytes 6148
  292.4 65.8 %copy-start.5 = (bf16[1792,16]{0,1:T(8,128)(2,1)S(1)}, bf16[1792,16]{0,1:T(8,128)(2,1)}, u32[]{:S(2)}) copy-start(bf16[1792,16]{0,1:T(8,128)(2,1)} %param.12) | copy-start | bytes 172036
  357.6 1.1 copy-start.3
